TPU v7x, 256 devices: a whole 4x4x8 slice. The times are simulated.
256 devices in a mesh: dp: 32 (over z, x_hi, core), owner: 8 (over x_lo, y).
Axes of the slice: x: 4 (x_hi: 2, x_lo: 2; x = x_hi * 2 + x_lo), y: 4, z: 8, core: 2. Of those that a mesh axis runs over, the one named last changes fastest.
Arguments:
- edge_in: bfloat16 [8, 65536, 512], P(None, ('dp', 'owner')), may hold values from -256 to 256
- edge_grad: bfloat16 [8, 65536, 512], P(None, ('dp', 'owner')), may hold values from -1.1953125 to 1.1953125
- row_mask: int32 [8, 65536], P(None, ('dp', 'owner')), may hold values 0 or 1
- layer_at: int32 [8], replicated, may hold values from 0 to 7, each once
Outputs:
- update: bfloat16 [8, 512, 512], P('owner')
Inputs may be any that keep to these rules, and one draw needn't show every extreme that they name: `layer_at`: every layer number appears once.
All inputs are finite; a program needn't handle non-finite values. No bound on the sum of `row_mask` on one device may be relied on, other than what follows from the above.
Results may differ from a plain program's by a relative error of at most 0.0085.
Values may be sent and summed in bfloat16 or wider, within the bound.
A program may use at most 64 MiB of HBM per device.

v0:
```python
import contextlib
import math

import jax
import jax.numpy as jnp
from jax import lax
from jax.experimental import pallas as pl
from jax.experimental.pallas import tpu as pltpu
from jax.sharding import PartitionSpec as P

MESH = pl.DeviceIdType.MESH
F32 = jnp.float32
BF16 = jnp.bfloat16
L = 8
D = 512
R = 256
NZ = 8
T = 128
UPPER = [(i, j) for i in range(4) for j in range(i, 4)]
NF = len(UPPER)
ZF = 7
YF = NF - ZF
ZP, YP = 16 * ZF, 16 * YF
GB = 16
HB = 4
XB = GB - HB
GP = 16 * GB


def add(a, b):
    return (a.astype(F32) + b.astype(F32)).astype(BF16)


def split(x):
    hi = x.astype(BF16)
    return hi, (x - hi.astype(F32)).astype(BF16)


def dot(a, b):
    return lax.dot_general(a, b, (((1,), (0,)), ((), ())), preferred_element_type=F32)


def dot3(a, b):
    (ah, al), (bh, bl) = a, b
    return dot(ah, bh) + (dot(ah, bl) + dot(al, bh))


def kernel(
    layer_at, mask_hbm, in_hbm, grad_hbm, out,
    mask, rows_in, rows_grad, dummy,
    WZ, RZ, VZ, RZr, RZd, XZ, XZr,
    WY0, RY0r, RY0d, WY1, RY1r, RY1d, XY, XYr, UY, RUr, RUd, HY, HYr, FZ, FY,
    WG, RGr, RGd, XG, XGr, WX, RX, VX, RXr, RXd, YX, UG, RUGr, RUGd, HG, HGr, GA,
    Fm, Pm, Qm, Gm, X, Xp, mine, local_sem, send_sem, recv_sem,
):
    dp, ow = lax.axis_index("dp"), lax.axis_index("owner")
    z, xh, c = dp // 4, (dp // 2) % 2, dp % 2
    xl, y = ow // 4, ow % 4

    def dev(z=z, xh=xh, c=c, xl=xl, y=y):
        return (z * 4 + xh * 2 + c, xl * 4 + y)

    ya = y + 1 - 2 * (y % 2)
    yb = 3 - y
    yo = (y + 2) % 4
    core = dev(c=1 - c)
    dev_ya, dev_yb = dev(y=ya), dev(y=yb)
    dev_x, dev_x2, dev_xh = dev(xl=1 - xl), dev(xl=1 - xl, xh=1 - xh), dev(xh=1 - xh)
    up, down = dev(z=(z + 1) % NZ), dev(z=(z + NZ - 1) % NZ)

    used = [0]
    groups, groupsG = [], []

    def ids():
        used[0] += 1
        return used[0] - 1

    def remote(src, dst, k, to, g=0):
        return pltpu.make_async_remote_copy(
            src_ref=src, dst_ref=dst, send_sem=send_sem.at[g], recv_sem=recv_sem.at[k],
            device_id=to, device_id_type=MESH,
        )

    def send(src, dst, k, to):
        size = math.prod(src.shape) * src.dtype.itemsize
        if not groups or groups[-1] + size > SENT:
            groups.append(0)
        groups[-1] += size
        remote(src, dst, k, to, len(groups) - 1).start()

    def sent(groups):
        for g, size in enumerate(groups):
            ref = dummy.at[pl.ds(0, size // (2 * D))]
            pltpu.make_async_copy(ref, ref, send_sem.at[g]).wait()
        assert len(groups) <= LAST, len(groups)

    def arrived(dst, k):
        remote(dst, dst, k, core).wait_recv()

    @contextlib.contextmanager
    def stage(name):
        with jax.named_scope(name):
            yield
        if FENCE:
            pl.delay(1)

    barrier = pltpu.get_barrier_semaphore()
    up2, down2 = dev(z=(z + 2) % NZ), dev(z=(z + NZ - 2) % NZ)
    peers = (core, dev_ya, dev_yb, dev_x, dev_x2, dev_xh, up, down, up2, down2)
    for peer in peers:
        pl.semaphore_signal(barrier, inc=1, device_id=peer, device_id_type=MESH)

    own, other = pl.ds(0, R), pl.ds(R, R)
    loads = ((mask_hbm, mask.at[:, own]), (in_hbm, rows_in.at[:, own, :]), (grad_hbm, rows_grad.at[:, own, :]))
    gets = [(mask_hbm, mask.at[:, other]), (in_hbm, rows_in.at[:, other, :]), (grad_hbm, rows_grad.at[:, other, :])]
    gets = [(src, dst, ids(), LAST + i) for i, (src, dst) in enumerate(gets)]
    for i, (src, dst) in enumerate(loads):
        pltpu.make_async_copy(src, dst, local_sem.at[i]).start()
    with stage("barrier"):
        pl.semaphore_wait(barrier, len(peers))
        for src, dst, k, g in gets:
            remote(src, dst, k, core, g).start()

    def loaded(i):
        src, dst = loads[i]
        pltpu.make_async_copy(src, dst, local_sem.at[i]).wait()
        arrived(gets[i][1], gets[i][2])

    with stage("waitA"):
        loaded(0)
        loaded(1)

    dirs = ((1, up, up2), (-1, down, down2))

    def zd(direction, far):
        return (z + NZ + direction * far) % NZ

    class ZRing:
        def __init__(self, W, Rz, rows, chunks):
            self.W, self.Rz = W, Rz
            self.k = [[ids() for _ in range(chunks)] for _ in range(4)]
            self.half = [pl.ds(0, rows // 2), pl.ds(rows // 2, rows // 2)]

        def go(self, n, s, q, half=None):
            w, r = self.W.at[zd(dirs[n][0], 4 - s), q], self.Rz.at[s, q, n]
            if half is not None:
                w, r = w.at[:, half, :], r.at[:, half, :]
            send(w, r, self.k[s][q], dirs[n][1])

        def start(self, q=0):
            for n in range(2):
                self.go(n, 0, q, self.half[n])
            for n in range(2):
                self.go(n, 1, q, self.half[1 - n])

        def step(self, s, q=0):
            arrived(self.Rz.at[s - 1, q, 0] if s == 1 else self.Rz.at[s - 1, q], self.k[s - 1][q])
            for n in range(2):
                d = zd(dirs[n][0], 4 - s)
                if s == 1:
                    h = self.half[n]
                    self.W[d, q, :, h, :] = add(self.W[d, q, :, h, :], self.Rz[0, q, n, :, h, :])
                    self.go(n, 1, q, h)
                else:
                    self.W[d, q] = add(self.W[d, q], self.Rz[s - 1, q, n])
                    self.go(n, s, q)

        def finish(self, q=0):
            arrived(self.Rz.at[3, q], self.k[3][q])
            mine = self.W[z, q].astype(F32)
            return (mine + (self.Rz[3, q, 0].astype(F32) + self.Rz[3, q, 1].astype(F32))).astype(BF16)

    class YStage:
        def __init__(self, W, Rr, Rd, rows):
            self.W, self.Rr, self.Rd = W, Rr, Rd
            self.kr, self.kd = ids(), ids()
            h = rows // 2
            self.half = [pl.ds(0, h), pl.ds(h, h)]

        def relay(self):
            for s, to in enumerate((dev_ya, dev_yb)):
                send(self.W.at[yo, :, self.half[s], :], self.Rr.at[s], self.kr, to)

        def direct(self, s):
            d, to = ((ya, dev_ya), (yb, dev_yb))[s]
            send(self.W.at[d, :, self.half[s], :], self.Rd.at[0, s], self.kd, to)

        def start(self):
            self.relay()
            self.direct(0)
            self.direct(1)

        def middle(self):
            arrived(self.Rr, self.kr)
            for s, (d, to) in enumerate(((yb, dev_yb), (ya, dev_ya))):
                h = self.half[s]
                self.W[d, :, h, :] = add(self.W[d, :, h, :], self.Rr[s])
                send(self.W.at[d, :, h, :], self.Rd.at[1, s], self.kd, to)

        def finish(self, out):
            arrived(self.Rd, self.kd)
            for s in range(2):
                h = self.half[s]
                total = self.W[y, :, h, :].astype(F32) + (self.Rd[0, s].astype(F32) + self.Rd[1, s].astype(F32))
                out[:, h, :] = total.astype(BF16)

    class ZPair:
        def __init__(self, W, Rr, Rd, rows):
            self.W, self.Rr, self.Rd, self.kr, self.kd = W, Rr, Rd, ids(), ids()
            self.half = [pl.ds(0, rows // 2), pl.ds(rows // 2, rows // 2)]

        def start(self):
            W, Rr = self.W, self.Rr
            for n, (direction, to, to2) in enumerate(dirs):
                send(W.at[zd(direction, 3), 0], Rr.at[n], self.kr, to)
                h = self.half[n]
                send(W.at[zd(direction, 4), 0, :, h, :], Rr.at[2, :, h, :], self.kr, to2)
            for n, (direction, to, to2) in enumerate(dirs):
                send(W.at[zd(direction, 1), 0], self.Rd.at[n], self.kd, to)

        def middle(self):
            W, Rr = self.W, self.Rr
            arrived(Rr, self.kr)
            for n, (direction, to, to2) in enumerate(dirs):
                d = zd(direction, 2)
                near, far = self.half[1 - n], self.half[n]
                W[d, 0, :, near, :] = add(W[d, 0, :, near, :], Rr[n, :, near, :])
                both = Rr[n, :, far, :].astype(F32) + Rr[2, :, far, :].astype(F32)
                W[d, 0, :, far, :] = (W[d, 0, :, far, :].astype(F32) + both).astype(BF16)
                send(W.at[d, 0], self.Rd.at[2 + n], self.kd, to2)

        def finish(self):
            Rd = self.Rd
            arrived(Rd, self.kd)
            near = Rd[0].astype(F32) + Rd[1].astype(F32)
            far = Rd[2].astype(F32) + Rd[3].astype(F32)
            return ((self.W[z, 0].astype(F32) + near) + far).astype(BF16)

    class AllGather:
        def __init__(self, A, rows):
            self.A, self.k = A, [ids() for _ in range(3)]
            self.half = [pl.ds(0, rows // 2), pl.ds(rows // 2, rows // 2)]

        def start(self):
            p = self.A.at[z]
            for direction, to, to2 in dirs:
                send(p, p, self.k[0], to)
            for direction, to, to2 in dirs:
                send(p, p, self.k[1], to2)

        def relay(self):
            arrived(self.A.at[pl.ds(0, 2)], self.k[1])
            for n, (direction, to, to2) in enumerate(dirs):
                p = self.A.at[zd(-direction, 2)]
                send(p, p, self.k[2], to)
            for n, (direction, to, to2) in enumerate(dirs):
                p = self.A.at[zd(-direction, 2), self.half[n], :]
                send(p, p, self.k[2], to2)

        def finish(self):
            arrived(self.A.at[pl.ds(0, 2)], self.k[0])
            arrived(self.A.at[pl.ds(0, 3)], self.k[2])

    order = (yo, ya, yb, y)
    fz = ZRing(WZ, RZ, ZP, 8)
    fzy = YStage(VZ, RZr, RZd, ZP)
    fy = (YStage(WY0, RY0r, RY0d, YF * T), YStage(WY1, RY1r, RY1d, YF * T))
    fyz = ZPair(UY, RUr, RUd, YP)
    faz = (AllGather(FZ.at[0], ZP), AllGather(FZ.at[1], ZP))
    fay = (AllGather(FY.at[0], YP), AllGather(FY.at[1], YP))
    gy = YStage(WG, RGr, RGd, HB * T)
    gxy = YStage(VX, RXr, RXd, XB * T)
    gz = ZPair(UG, RUGr, RUGd, GP)
    ga = AllGather(GA, GP)
    k_fx = [ids() for _ in range(2)]
    k_gx = [ids() for _ in range(4)]
    k_xz, k_fh, k_gh, k_xg = (ids() for _ in range(4))
    k_fpz, k_fpy, k_gp, k_x, k_out = (ids() for _ in range(5))

    def pieces(ref, m, first, f, n):
        for k in range(n):
            ref[:, 0, m, 16 * (first + k) : 16 * (first + k + 1), :] = f[k * T : (k + 1) * T].reshape(8, 16, T)

    def factor(i, x):
        f, t = i // 4, i % 4
        d = order[t]
        layer = layer_at[x * 4 + d]
        a = (rows_in, rows_grad)[f][layer]
        m = mask[pl.ds(layer, 1), :].astype(F32).astype(BF16)
        am = a.T * m
        top = dot(am[:R], a) * (1.0 / 65536)
        low = dot(am[R:], a[:, R:]) * (1.0 / 65536)
        for k, (p, q) in enumerate(UPPER):
            if p < 2:
                block = top[p * T : (p + 1) * T, q * T : (q + 1) * T].astype(BF16)
            else:
                block = low[(p - 2) * T : (p - 1) * T, (q - 2) * T : (q - 1) * T].astype(BF16)
            if k < ZF:
                WZ[:, i, x, 16 * k : 16 * (k + 1), :] = block.reshape(8, 16, T)
            else:
                (WY0, WY1)[f][d, x, (k - ZF) * T : (k - ZF + 1) * T, :] = block

    def gradient(t, x):
        d = order[t]
        layer = layer_at[x * 4 + d]
        g = (dot(rows_in[layer].T, rows_grad[layer]) * (1.0 / 256)).astype(BF16)
        for k in range(GB):
            p, q = k // 4, k % 4
            block = g[p * T : (p + 1) * T, q * T : (q + 1) * T]
            if k < HB:
                WG[d, x, k * T : (k + 1) * T, :] = block
            else:
                WX[x, d, (k - HB) * T : (k - HB + 1) * T, :] = block

    def both(f, t):
        lax.fori_loop(0, 2, lambda x, carry: (f(t, x), carry)[1], 0)

    def leave(ystage, t):
        if t == 0:
            ystage.relay()
        elif t < 3:
            ystage.direct(t - 1)

    def halves(rows):
        return (pl.ds(0, rows // 2), dev_x), (pl.ds(rows // 2, rows // 2), dev_x2)


    @pl.when(c == 1)
    def _():
        def fx(f):
            with stage("fyfin"):
                fy[f].finish(XY.at[f])
                for h, to in halves(YF * T):
                    send(XY.at[f, 1 - xl, h, :], XYr.at[f, h, :], k_fx[f], to)

        for i in range(8 + 3 * LAG):
            if i < 8:
                f, t = i // 4, i % 4
                with stage(f"factor{i}"):
                    if i == 4:
                        loaded(2)
                    both(factor, i)
                    fz.start(i)
                    leave(fy[f], t)
            for s in (3, 2, 1):
                if 0 <= i - s * LAG < 8:
                    with stage(f"fz{s}"):
                        fz.step(s, i - s * LAG)
            if i == 4:
                with stage("fy0mid"):
                    fy[0].middle()
            if i == 8:
                with stage("fy1mid"):
                    fy[1].middle()
            if i in AT_FX:
                fx(AT_FX.index(i))
        with stage("fxfin"):
            for f in range(2):
                arrived(XYr.at[f], k_fx[f])
                pieces(UY, f, 0, add(XY[f, xl], XYr[f]), YF)
            fyz.start()
        for t in range(4):
            with stage("fzfin"):
                for f in range(2):
                    v = fz.finish(4 * f + t)
                    for x in range(2):
                        VZ[order[t], 2 * x + f] = v[x]
                leave(fzy, t)
        with stage("fyzmid"):
            fyz.middle()
        with stage("fzymid"):
            fzy.middle()
        with stage("fyzfin"):
            HY[...] = fyz.finish()
            send(HY, HYr, k_fh, dev_xh)
        with stage("fzyfin"):
            fzy.finish(XZ)
            theirs = XZ.at[pl.ds(2 * (1 - xl), 2)]
            send(theirs, XZr.at[0], k_xz, dev_x)
            send(theirs, XZr.at[1], k_xz, dev_x2)
            send(XZ.at[pl.ds(2 * xl, 2)], XZr.at[2], k_xz, dev_xh)
        with stage("fhfin"):
            arrived(HYr, k_fh)
            FY[:, z] = add(HY[...], HYr[...])
            fay[0].start()
            fay[1].start()
        with stage("fxm"):
            arrived(XZr, k_xz)
            near = XZr[0].astype(F32) + XZr[1].astype(F32)
            FZ[:, z] = ((XZ[pl.ds(2 * xl, 2)].astype(F32) + XZr[2].astype(F32)) + near).astype(BF16)
            faz[0].start()
            faz[1].start()
        with stage("fayrelay"):
            fay[0].relay()
            fay[1].relay()
        with stage("fazrelay"):
            faz[0].relay()
            faz[1].relay()
        with stage("fafin"):
            fay[0].finish()
            send(FY.at[0], FY.at[0], k_fpy, core)
            faz[0].finish()
            send(FZ.at[0], FZ.at[0], k_fpz, core)
            fay[1].finish()
            faz[1].finish()

    @pl.when(c == 0)
    def _():
        kept, groups[:] = list(groups), []
        with stage("waitB"):
            loaded(2)
        for t in range(4):
            with stage("grad"):
                both(gradient, t)
                d = order[t]
                for h, to in halves(XB * T):
                    send(WX.at[1 - xl, d, h, :], RX.at[d, h, :], k_gx[t], to)
                leave(gy, t)
        for t in range(4):
            with stage("gx"):
                d = order[t]
                arrived(RX.at[d], k_gx[t])
                VX[d, 0] = add(WX[xl, d], RX[d])
                leave(gxy, t)
            if t == 1:
                with stage("gymid"):
                    gy.middle()
            if t == 2:
                with stage("gxymid"):
                    gxy.middle()
        with stage("gyfin"):
            gy.finish(XG)
            for h, to in halves(HB * T):
                send(XG.at[1 - xl, h, :], XGr.at[h, :], k_xg, to)
        with stage("gxyfin"):
            gxy.finish(YX)
            pieces(UG, 0, HB, YX[0], XB)
        with stage("gxfin"):
            arrived(XGr, k_xg)
            pieces(UG, 0, 0, add(XG[xl], XGr[...]), HB)
            gz.start()
        with stage("gzmid"):
            gz.middle()
        with stage("gzfin"):
            HG[...] = gz.finish()[0]
            send(HG, HGr, k_gh, dev_xh)
        with stage("ghfin"):
            arrived(HGr, k_gh)
            GA[z] = add(HG[...], HGr[...])
            ga.start()
        with stage("waitF"):
            arrived(FY.at[0], k_fpy)
            arrived(FZ.at[0], k_fpz)
        groupsG.extend(groups)
        groups[:] = kept

    with stage("damp"):
        for k, (p, q) in enumerate(UPPER):
            if k < ZF:
                block = FZ[c, :, 16 * k : 16 * (k + 1), :]
            else:
                block = FY[c, :, 16 * (k - ZF) : 16 * (k - ZF + 1), :]
            block = block.reshape(T, T).astype(F32)
            Fm[p * T : (p + 1) * T, q * T : (q + 1) * T] = block
            if p != q:
                Fm[q * T : (q + 1) * T, p * T : (p + 1) * T] = block.T
        eye = (
            lax.broadcasted_iota(jnp.int32, (D, D), 0) == lax.broadcasted_iota(jnp.int32, (D, D), 1)
        ).astype(F32)
        f = Fm[...]
        trace = jnp.sum(jnp.sum(f * eye, axis=0, keepdims=True), axis=1, keepdims=True)
        damped = f + (trace * (0.05 / D)) * eye
        square = jnp.sum(jnp.sum(damped * damped, axis=0, keepdims=True), axis=1, keepdims=True)
        inverse_size = 1.0 / jnp.sqrt(square + 1e-06)
        Pm[...] = eye - damped * inverse_size

    with stage("ns1"):
        r = split(Pm[...])
        Fm[...] = dot3(r, r)
    @pl.when(c == 0)
    def _():
        kept, groups[:] = list(groups), groupsG
        with stage("garelay"):
            ga.relay()
        groupsG[:], groups[:] = list(groups), kept

    with stage("ns2"):
        r1 = split(Fm[...])
        Qm[...] = dot3(r1, r1)

    with stage("ns3"):
        Pm[...] = eye + Pm[...] + Fm[...] + dot3(r, r1)

    with stage("ns4"):
        r2 = split(Qm[...])
        Fm[...] = dot3(r2, r2)
        Pm[...] = Pm[...] + dot3(split(Pm[...]), r2)

    @pl.when(c == 0)
    def _():
        with stage("gafin"):
            ga.finish()
            remote(GA, GA, k_gp, core, LAST + 5).start()

    with stage("ns5"):
        r3 = split(Fm[...])
        X[0], X[1] = split((Pm[...] + dot3(split(Pm[...]), r3)) * inverse_size)

    lo, hi = pl.ds(0, R), pl.ds(R, R)
    out_lo, out_hi = out.at[0, lo, :], out.at[0, hi, :]

    def gather():
        for k in range(GB):
            p, q = k // 4, k % 4
            Gm[p * T : (p + 1) * T, q * T : (q + 1) * T] = GA[:, 16 * k : 16 * (k + 1), :].reshape(T, T)

    @pl.when(c == 1)
    def _():
        remote(X, Xp, k_x, core, LAST + 3).start()
        with stage("waitG"):
            arrived(GA, k_gp)
        with stage("gather"):
            gather()
            right = split(dot(Gm[...], X[0]) + dot(Gm[...], X[1]))
        with stage("waitX"):
            arrived(Xp.at[:, hi, :], k_x)
        with stage("last"):
            mine[...] = dot3((Xp[0, hi, :], Xp[1, hi, :]), right).astype(BF16)
            remote(mine, out_hi, k_out, core, LAST + 4).start()
            pltpu.make_async_copy(mine, out_hi, local_sem.at[3]).start()
        with stage("drain"):
            remote(X, Xp, k_x, core, LAST + 3).wait_send()
            sent(groups)

    @pl.when(c == 0)
    def _():
        theirs = X.at[:, hi, :], Xp.at[:, hi, :]
        remote(*theirs, k_x, core, LAST + 3).start()
        with stage("gather"):
            gather()
            left = split(dot(X[0, lo, :], Gm[...]) + dot(X[1, lo, :], Gm[...]))
        with stage("waitX"):
            arrived(Xp, k_x)
        with stage("last"):
            mine[...] = dot3(left, (Xp[0], Xp[1])).astype(BF16)
            remote(mine, out_lo, k_out, core, LAST + 4).start()
            pltpu.make_async_copy(mine, out_lo, local_sem.at[3]).start()
        with stage("drain"):
            remote(*theirs, k_x, core, LAST + 3).wait_send()
            remote(GA, GA, k_gp, core, LAST + 5).wait_send()
            sent(groupsG)

    with stage("waitO"):
        pltpu.make_async_copy(mine, out_lo, local_sem.at[3]).wait()
        arrived(out_lo, k_out)
        remote(mine, out_lo, k_out, core, LAST + 4).wait_send()
        for src, dst, k, g in gets:
            remote(src, dst, k, core, g).wait_send()
    assert used[0] == NSEM, used[0]


FENCE = True
LAG = 3
AT_FX = (9, 12)
SENT = 2 * 1024 * 1024
NSEM = 79
LAST = 6
NSEND = LAST + 6


def local_step(edge_in, edge_grad, row_mask, layer_at):
    def v(*shape, dtype=BF16):
        return pltpu.VMEM(shape, dtype)

    def ystage(m, rows):
        return [v(4, m, rows, T), v(2, m, rows // 2, T), v(2, 2, m, rows // 2, T)]

    def zpair(m, rows):
        return [v(NZ, 1, m, rows, T), v(3, m, rows, T), v(4, m, rows, T)]

    def zring(chunks, m, rows):
        return [v(NZ, chunks, m, rows, T), v(4, chunks, 2, m, rows, T)]

    yf, hb, xb = YF * T, HB * T, XB * T
    any_ = pl.BlockSpec(memory_space=pl.ANY)
    return pl.pallas_call(
        kernel,
        out_shape=jax.ShapeDtypeStruct((1, D, D), BF16),
        in_specs=[pl.BlockSpec(memory_space=pltpu.SMEM), any_, any_, any_],
        out_specs=any_,
        scratch_shapes=[
            v(L, 2 * R, dtype=jnp.int32), v(L, 2 * R, D), v(L, 2 * R, D), v(SENT // (2 * D), D),
            *zring(8, 2, ZP), *ystage(4, ZP), v(4, ZP, T), v(3, 2, ZP, T),
            *ystage(2, yf), *ystage(2, yf), v(2, 2, yf, T), v(2, yf, T), *zpair(2, YP), v(2, YP, T), v(2, YP, T),
            v(2, NZ, ZP, T), v(2, NZ, YP, T),
            *ystage(2, hb), v(2, hb, T), v(hb, T), v(2, 4, xb, T), v(4, xb, T), *ystage(1, xb), v(1, xb, T),
            *zpair(1, GP), v(GP, T), v(GP, T), v(NZ, GP, T),
            v(D, D, dtype=F32), v(D, D, dtype=F32), v(D, D, dtype=F32), v(D, D), v(2, D, D), v(2, D, D), v(R, D),
            pltpu.SemaphoreType.DMA((4,)), pltpu.SemaphoreType.DMA((NSEND,)), pltpu.SemaphoreType.DMA((NSEM,)),
        ],
        compiler_params=pltpu.CompilerParams(
            collective_id=0, has_side_effects=True, vmem_limit_bytes=60 * 1024 * 1024
        ),
    )(layer_at, row_mask, edge_in, edge_grad)


def solution(mesh):
    rows = P(None, ("dp", "owner"), None)
    return jax.shard_map(
        local_step, mesh=mesh, in_specs=(rows, rows, P(None, ("dp", "owner")), P()),
        out_specs=P("owner", None, None), check_vma=False,
    )
```

profile of v0, /device:TPU:1, one launch (start us, length us, event | category | flops | bytes accessed | tf_op | source)
XLA Modules:
  0.0 68.0 jit_solution(15617282464283593074)
XLA Ops:
  0.0 66.1 %shard_map.46 = bf16[1,512,512]{2,1,0:T(8,128)(2,1)} custom-call(s32[8]{0:T(128)} %layer_at.1, s32[8,256]{1,0:T(8,128)} %mask_hbm.1, bf16[8,256,512]{2,1,0:T(8,128)(2,1)} %in_hbm.1, bf16[8,256,512]{2,1,0:T(8,128)(2,1)} %grad_hbm.1), custom_call_target="tpu_custom_call" | custom-call | tf_op jit(solution)/shard_map/pallas_call | solution.py:586
  66.1 1.9 %copy.6 = bf16[1,512,512]{2,1,0:T(8,128)(2,1)} copy(bf16[1,512,512]{2,1,0:T(8,128)(2,1)} %shard_map.46) | data formatting | bytes 1048576
where the time goes:
time: 68.1 us; the launch traced here: 68 us
  Pallas kernels  66.1 us (97%)
  local copies, waits for them, and re-layouts  1.87 us (3%)
    pallas_call x1, Pallas kernels, local_step(): pl.pallas_call(kernel, out_shape=jax.ShapeDtypeStruct((1, D, D), BF16), i...  66.1 us
    unnamed x1, local copies, waits for them, and re-layouts  1.87 us

commit v1 on v0

--- a/solution.py
+++ b/solution.py
@@ -212,9 +212,9 @@
         def start(self):
             W, Rr = self.W, self.Rr
             for n, (direction, to, to2) in enumerate(dirs):
-                send(W.at[zd(direction, 3), 0], Rr.at[n], self.kr, to)
                 h = self.half[n]
                 send(W.at[zd(direction, 4), 0, :, h, :], Rr.at[2, :, h, :], self.kr, to2)
+                send(W.at[zd(direction, 3), 0], Rr.at[n], self.kr, to)
             for n, (direction, to, to2) in enumerate(dirs):
                 send(W.at[zd(direction, 1), 0], self.Rd.at[n], self.kd, to)
 
@@ -244,18 +244,18 @@
         def start(self):
             p = self.A.at[z]
             for direction, to, to2 in dirs:
+                send(p, p, self.k[1], to2)
+            for direction, to, to2 in dirs:
                 send(p, p, self.k[0], to)
-            for direction, to, to2 in dirs:
-                send(p, p, self.k[1], to2)
 
         def relay(self):
             arrived(self.A.at[pl.ds(0, 2)], self.k[1])
             for n, (direction, to, to2) in enumerate(dirs):
+                p = self.A.at[zd(-direction, 2), self.half[n], :]
+                send(p, p, self.k[2], to2)
+            for n, (direction, to, to2) in enumerate(dirs):
                 p = self.A.at[zd(-direction, 2)]
                 send(p, p, self.k[2], to)
-            for n, (direction, to, to2) in enumerate(dirs):
-                p = self.A.at[zd(-direction, 2), self.half[n], :]
-                send(p, p, self.k[2], to2)
 
         def finish(self):
             arrived(self.A.at[pl.ds(0, 2)], self.k[0])

time: 68.1 us -> 66.7 us (0.979)
  Pallas kernels: 66.1 us -> 64.7 us
    pallas_call x1, Pallas kernels: 66.1 us -> 64.7 us  [local_step(): pl.pallas_call(kernel, out_shape=jax.ShapeDtypeStruct((1, D, D), BF16), i...]
where the time goes in v1:
time: 66.7 us; the launch traced here: 66.5 us
  Pallas kernels  64.7 us (97%)
  local copies, waits for them, and re-layouts  1.87 us (3%)
    pallas_call x1, Pallas kernels, local_step(): pl.pallas_call(kernel, out_shape=jax.ShapeDtypeStruct((1, D, D), BF16), i...  64.7 us
    unnamed x1, local copies, waits for them, and re-layouts  1.87 us

profile of v1, /device:TPU:1, one launch (start us, length us, event | category | flops | bytes accessed | tf_op | source)
XLA Modules:
  0.0 66.5 jit_solution(1688093403316801906)
XLA Ops:
  0.0 64.7 %shard_map.46 = bf16[1,512,512]{2,1,0:T(8,128)(2,1)} custom-call(s32[8]{0:T(128)} %layer_at.1, s32[8,256]{1,0:T(8,128)} %mask_hbm.1, bf16[8,256,512]{2,1,0:T(8,128)(2,1)} %in_hbm.1, bf16[8,256,512]{2,1,0:T(8,128)(2,1)} %grad_hbm.1), custom_call_target="tpu_custom_call" | custom-call | tf_op jit(solution)/shard_map/pallas_call | solution.py:586
  64.7 1.9 %copy.6 = bf16[1,512,512]{2,1,0:T(8,128)(2,1)} copy(bf16[1,512,512]{2,1,0:T(8,128)(2,1)} %shard_map.46) | data formatting | bytes 1048576

commit v2 on v1

--- a/solution.py
+++ b/solution.py
@@ -482,6 +482,9 @@
         kept, groups[:] = list(groups), groupsG
         with stage("garelay"):
             ga.relay()
+            arrived(GA.at[pl.ds(0, 2)], ga.k[0])
+            for far in (0, 1, 2, 6, 7):
+                remote(GA.at[(z + far) % NZ], GA.at[(z + far) % NZ], k_gp, core, LAST + 5).start()
         groupsG[:], groups[:] = list(groups), kept
 
     with stage("ns2"):
@@ -499,8 +502,9 @@
     @pl.when(c == 0)
     def _():
         with stage("gafin"):
-            ga.finish()
-            remote(GA, GA, k_gp, core, LAST + 5).start()
+            arrived(GA.at[pl.ds(0, 3)], ga.k[2])
+            for far in (3, 4, 5):
+                remote(GA.at[(z + far) % NZ], GA.at[(z + far) % NZ], k_gp, core, LAST + 5).start()
 
     with stage("ns5"):
         r3 = split(Fm[...])
@@ -585,7 +589,7 @@
     any_ = pl.BlockSpec(memory_space=pl.ANY)
     return pl.pallas_call(
         kernel,
-        out_shape=jax.ShapeDtypeStruct((1, D, D), BF16),
+        out_shape=pltpu.VMEM((1, D, D), BF16),
         in_specs=[pl.BlockSpec(memory_space=pltpu.SMEM), any_, any_, any_],
         out_specs=any_,
         scratch_shapes=[

time: 66.7 us -> 65.5 us (0.982)
  local copies, waits for them, and re-layouts: 1.87 us -> 0.8 us
    unnamed x1, local copies, waits for them, and re-layouts: 1.87 us -> 0.8 us
where the time goes in v2:
time: 65.5 us; the launch traced here: 65.4 us
  Pallas kernels  64.6 us (99%)
  local copies, waits for them, and re-layouts  0.8 us (1%)
    pallas_call x1, Pallas kernels, local_step(): pl.pallas_call(kernel, out_shape=pltpu.VMEM((1, D, D), BF16), in_specs=[p...  64.6 us

profile of v2, /device:TPU:1, one launch (start us, length us, event | category | flops | bytes accessed | tf_op | source)
XLA Modules:
  0.0 65.4 jit_solution(9371828686101920356)
XLA Ops:
  0.0 64.6 %shard_map.46 = bf16[1,512,512]{2,1,0:T(8,128)(2,1)S(1)} custom-call(s32[8]{0:T(128)} %layer_at.1, s32[8,256]{1,0:T(8,128)} %mask_hbm.1, bf16[8,256,512]{2,1,0:T(8,128)(2,1)} %in_hbm.1, bf16[8,256,512]{2,1,0:T(8,128)(2,1)} %grad_hbm.1), custom_call_target="tpu_custom_call" | custom-call | tf_op jit(solution)/shard_map/pallas_call | solution.py:590
  64.6 0.8 %copy.6 = bf16[1,512,512]{2,1,0:T(8,128)(2,1)} copy(bf16[1,512,512]{2,1,0:T(8,128)(2,1)S(1)} %shard_map.46) | data formatting | bytes 1048576

commit v3 on v2

--- a/solution.py
+++ b/solution.py
@@ -38,6 +38,10 @@
 
 def dot(a, b):
     return lax.dot_general(a, b, (((1,), (0,)), ((), ())), preferred_element_type=F32)
+
+
+def stack(a, b):
+    return tuple(jnp.concatenate(p, axis=0) for p in zip(a, b))
 
 
 def dot3(a, b):
@@ -489,15 +493,15 @@
 
     with stage("ns2"):
         r1 = split(Fm[...])
-        Qm[...] = dot3(r1, r1)
-
-    with stage("ns3"):
-        Pm[...] = eye + Pm[...] + Fm[...] + dot3(r, r1)
+        two = dot3(stack(r1, r), r1)
+        Qm[...] = two[:D]
+        Pm[...] = eye + Pm[...] + Fm[...] + two[D:]
 
     with stage("ns4"):
         r2 = split(Qm[...])
-        Fm[...] = dot3(r2, r2)
-        Pm[...] = Pm[...] + dot3(split(Pm[...]), r2)
+        two = dot3(stack(r2, split(Pm[...])), r2)
+        Fm[...] = two[:D]
+        Pm[...] = Pm[...] + two[D:]
 
     @pl.when(c == 0)
     def _():

time: 65.5 us -> 65.4 us (level)
  no operation moved by 1% of the time
where the time goes in v3:
time: 65.4 us; the launch traced here: 65.3 us
  Pallas kernels  64.5 us (99%)
  local copies, waits for them, and re-layouts  0.8 us (1%)
    pallas_call x1, Pallas kernels, local_step(): pl.pallas_call(kernel, out_shape=pltpu.VMEM((1, D, D), BF16), in_specs=[p...  64.5 us

profile of v3, /device:TPU:1, one launch (start us, length us, event | category | flops | bytes accessed | tf_op | source)
XLA Modules:
  0.0 65.3 jit_solution(14416535464815146113)
XLA Ops:
  0.0 64.5 %shard_map.46 = bf16[1,512,512]{2,1,0:T(8,128)(2,1)S(1)} custom-call(s32[8]{0:T(128)} %layer_at.1, s32[8,256]{1,0:T(8,128)} %mask_hbm.1, bf16[8,256,512]{2,1,0:T(8,128)(2,1)} %in_hbm.1, bf16[8,256,512]{2,1,0:T(8,128)(2,1)} %grad_hbm.1), custom_call_target="tpu_custom_call" | custom-call | tf_op jit(solution)/shard_map/pallas_call | solution.py:594
  64.5 0.8 %copy.6 = bf16[1,512,512]{2,1,0:T(8,128)(2,1)} copy(bf16[1,512,512]{2,1,0:T(8,128)(2,1)S(1)} %shard_map.46) | data formatting | bytes 1048576
